TPU v7x, 32 devices: a whole 2x2x4 slice. The times are simulated.
32 devices in a mesh: gx: 8 (over z, x), gy: 4 (over y, core).
Axes of the slice: x: 2, y: 2, z: 4, core: 2. Of those that a mesh axis runs over, the one named last changes fastest.
Arguments:
- velocity: float32 [2, 1024, 1024], P(None, 'gy', 'gx'), may hold values from -3 to 3
- stress: float32 [3, 1024, 1024], P(None, 'gy', 'gx'), may hold values from -3 to 3
- ice_mass: float32 [1024, 1024], P('gy', 'gx'), may hold values from 0.5 to 4
- strength: float32 [1024, 1024], P('gy', 'gx'), may hold values from 0.2 to 2
- land_mask: int32 [1024, 1024], P('gy', 'gx'), may hold values from 0 to 1
- ocean_forcing: float32 [4, 1024, 1024], P(None, ('gy', 'gx')), may hold values from -3 to 3
Outputs:
- velocity_out: float32 [2, 1024, 1024], P(None, 'gy', 'gx')
- stress_out: float32 [3, 1024, 1024], P(None, 'gy', 'gx')
- residuals: float32 [4], replicated
- ocean_stress: float32 [2, 1024, 1024], P(None, ('gy', 'gx'))
All inputs are finite; a program needn't handle non-finite values.
Results may differ from a plain program's by a relative error of at most 0.0001.
Values sent between devices are 32-bit elements; how exact they have to be, the bound alone decides.
A program may use at most 64 MiB of HBM per device.

v0:
```python
import jax
import jax.numpy as jnp
from jax import lax
from jax.sharding import PartitionSpec as P

ITERS = 4
ALPHA = 4.0
BETA = 4.0
WATER_DRAG = 1.0
DELTA_FLOOR = 0.0025


def extended(cells, sides, width):
    for axis, dim in sides:
        count = lax.axis_size(axis)
        head = lax.slice_in_dim(cells, 0, width, axis=dim)
        tail = lax.slice_in_dim(cells, cells.shape[dim] - width, cells.shape[dim], axis=dim)
        cells = jnp.concatenate(
            [
                lax.ppermute(tail, axis, [(i, (i + 1) % count) for i in range(count)]),
                cells,
                lax.ppermute(head, axis, [((i + 1) % count, i) for i in range(count)]),
            ],
            axis=dim,
        )
    return cells


def diff_east(padded):
    return 0.5 * (padded[..., 1:-1, 2:] - padded[..., 1:-1, :-2])


def diff_north(padded):
    return 0.5 * (padded[..., 2:, 1:-1] - padded[..., :-2, 1:-1])


def trim_edges(field, level):
    if level == 0:
        return field
    return field[..., level:-level, level:-level]


def record_sum(own_sum, global_sums):
    global_sums.append(lax.psum(own_sum, ("gx", "gy")))


def relax_stress(padded_vel, stress, strength, ice_frac):
    east_dx = diff_east(padded_vel[0])
    east_dy = diff_north(padded_vel[0])
    north_dx = diff_east(padded_vel[1])
    north_dy = diff_north(padded_vel[1])
    divergence = east_dx + north_dy
    tension = east_dx - north_dy
    shear_rate = east_dy + north_dx
    delta_rate = jnp.sqrt(
        divergence * divergence + 0.25 * (tension * tension + shear_rate * shear_rate) + DELTA_FLOOR
    )
    target = jnp.stack(
        [
            strength * (divergence / delta_rate - 1.0),
            strength * tension / (4.0 * delta_rate),
            strength * shear_rate / (8.0 * delta_rate),
        ]
    )
    return (stress + (target - stress) / ALPHA) * ice_frac


def drag_coeff(vel, currents):
    east_gap = currents[0] - vel[0]
    north_gap = currents[1] - vel[1]
    return WATER_DRAG * jnp.sqrt(east_gap * east_gap + north_gap * north_gap + 0.01)


def relax_velocity(padded_stress, vel, vel_start, forcing, ice_mass, coriolis, ice_frac):
    normal_xx = 0.5 * (padded_stress[0] + padded_stress[1])
    normal_yy = 0.5 * (padded_stress[0] - padded_stress[1])
    shear_xy = padded_stress[2]
    force_east = diff_east(normal_xx) + diff_north(shear_xy)
    force_north = diff_east(shear_xy) + diff_north(normal_yy)
    drag_rate = drag_coeff(vel, forcing[2:4])
    denominator = BETA + 1.0 + drag_rate / ice_mass
    new_east = (
        (
            BETA * vel[0]
            + vel_start[0]
            + (force_east + forcing[0] + drag_rate * forcing[2]) / ice_mass
            + coriolis * vel[1]
        )
        / denominator
        * ice_frac
    )
    new_north = (
        (
            BETA * vel[1]
            + vel_start[1]
            + (force_north + forcing[1] + drag_rate * forcing[3]) / ice_mass
            - coriolis * vel[0]
        )
        / denominator
        * ice_frac
    )
    return jnp.stack([new_east, new_north])


def local(velocity, stress, ice_mass, strength, land_mask, ocean_forcing):
    row_count = velocity.shape[1]
    col_count = velocity.shape[2]
    forcing = lax.all_to_all(ocean_forcing, "gx", split_axis=2, concat_axis=1, tiled=True)
    ice_frac = land_mask.astype(jnp.float32)
    lat_band = lax.axis_index("gy")
    total_rows = lax.axis_size("gy") * row_count
    global_sums = []
    depth = 2 * ITERS
    stacked = jnp.concatenate(
        [velocity, stress, strength[None], ice_mass[None], ice_frac[None], forcing], axis=0
    )
    padded = extended(stacked, (("gx", 2), ("gy", 1)), depth)
    wide_rows = lat_band * row_count - depth + jnp.arange(row_count + 2 * depth, dtype=jnp.int32)
    inside = ((wide_rows >= 0) & (wide_rows < total_rows)).astype(jnp.float32)[:, None]
    wide_vel = padded[0:2] * inside
    wide_stress = padded[2:5] * inside
    wide_strength = padded[5]
    wide_mass = padded[6]
    wide_ice = padded[7] * inside
    wide_forcing = padded[8:12]
    wide_lat = wide_rows.astype(jnp.float32)
    wide_coriolis = jnp.broadcast_to(
        (0.3 + 1.2 * (wide_lat + 0.5) / total_rows)[:, None],
        (row_count + 2 * depth, col_count + 2 * depth),
    )
    vel_work = wide_vel
    stress_work = wide_stress
    margin = depth
    for subcycle in range(ITERS):
        level_one = depth - (margin - 1)
        stress_cut = (stress_work.shape[-1] - (col_count + 2 * (margin - 1))) // 2
        stress_work = relax_stress(
            vel_work,
            trim_edges(stress_work, stress_cut),
            trim_edges(wide_strength, level_one),
            trim_edges(wide_ice, level_one),
        )
        level_two = depth - (margin - 2)
        old_vel = trim_edges(vel_work, 2)
        new_vel = relax_velocity(
            stress_work,
            old_vel,
            trim_edges(wide_vel, level_two),
            trim_edges(wide_forcing, level_two),
            trim_edges(wide_mass, level_two),
            trim_edges(wide_coriolis, level_two),
            trim_edges(wide_ice, level_two),
        )
        change = trim_edges(new_vel - old_vel, margin - 2)
        record_sum(jnp.sum(change * change), global_sums)
        vel_work = new_vel
        margin = margin - 2
    stress = trim_edges(stress_work, 1)
    history = jnp.stack(global_sums)
    drag_rate = drag_coeff(vel_work, forcing[2:4])
    ice_stress = drag_rate * (vel_work - forcing[2:4]) * ice_frac
    ocean_stress = lax.all_to_all(ice_stress, "gx", split_axis=1, concat_axis=2, tiled=True)
    return (vel_work, stress, history, ocean_stress)


def solution(mesh):
    placed = (
        P(None, "gy", "gx"),
        P(None, "gy", "gx"),
        P("gy", "gx"),
        P("gy", "gx"),
        P("gy", "gx"),
        P(None, ("gy", "gx"), None),
    )
    return jax.shard_map(
        local,
        mesh=mesh,
        in_specs=placed,
        out_specs=(P(None, "gy", "gx"), P(None, "gy", "gx"), P(), P(None, ("gy", "gx"), None)),
        check_vma=False,
    )
```

profile of v0, /device:TPU:0, one launch (start us, length us, event | category | flops | bytes accessed | tf_op | source)
XLA Modules:
  0.0 124.1 jit_solution(12943327118963534328)
XLA Ops:
  0.6 1.8 %copy.37 = f32[4,32,1024]{1,0,2:T(4,128)S(1)} copy(f32[4,32,1024]{2,1,0:T(8,128)} %param.11) | data formatting | bytes 1048576 | tf_op args[5]
  2.4 2.2 %reshape.95 = f32[8,1,16384]{2,1,0:T(1,128)} reshape(f32[1024,4,32]{2,1,0:T(4,128)S(1)} %bitcast.395) | data formatting | bytes 1048576
  4.6 7.4 %all-to-all-start = ((f32[8,1,16384]{2,1,0:T(1,128)}), f32[8,1,16384]{2,1,0:T(1,128)S(1)}, u32[]{:S(2)}, u32[]{:S(2)}) async-start(f32[8,1,16384]{2,1,0:T(1,128)} %reshape.95), calls=%async_computation | async-start | bytes 1048576 | tf_op jit(solution)/shard_map/all_to_all | solution.py:108
  12.2 1.0 constant_dynamic-update-slice_fusion.2
  13.5 13.0 %all-to-all-done = f32[8,1,16384]{2,1,0:T(1,128)S(1)} async-done(((f32[8,1,16384]{2,1,0:T(1,128)}), f32[8,1,16384]{2,1,0:T(1,128)S(1)}, u32[]{:S(2)}, u32[]{:S(2)}) %all-to-all-start) | async-done | bytes 524320 | tf_op jit(solution)/shard_map/all_to_all | solution.py:108
  27.0 1.9 %reduce.6 = f32[8,16384]{1,0:T(8,128)S(1)} reduce(f32[8,1,16384]{2,1,0:T(1,128)S(1)} %all-to-all-done, f32[]{:T(128)} %broadcast.256), dimensions={1}, to_apply=%all_to_all.26.reduce_sub_computation | reduce | bytes 1048580 | tf_op jit(solution)/shard_map/all_to_all | solution.py:108
  28.9 2.4 %reshape.96 = f32[1024,4,32]{2,1,0:T(4,128)} reshape(f32[8,16384]{1,0:T(8,128)S(1)} %reduce.6) | data formatting | bytes 1048576
  31.3 1.8 %copy.52 = f32[4,32,8,128]{3,1,2,0:T(8,128)S(1)} copy(f32[4,32,8,128]{1,0,3,2:T(4,128)} %bitcast.377) | data formatting | bytes 1048576 | tf_op jit(solution)/shard_map/all_to_all | solution.py:108
  33.2 1.7 %fusion.160 = (f32[12,256,8]{2,1,0:T(8,128)S(1)}, f32[12,256,8]{2,1,0:T(8,128)}) fusion(f32[12,256,128]{2,1,0:T(8,128)S(1)} %constant_dynamic-update-slice_fusion), kind=kLoop, calls=%fused_computation.288 | loop fusion | bytes 393216 | tf_op jit(solution)/shard_map/slice | solution.py:17
  34.9 1.8 %copy.41 = f32[12,256,8]{1,2,0:T(8,128)S(1)} copy(f32[12,256,8]{2,1,0:T(8,128)} %get-tuple-element.42) | data formatting | bytes 196608 | tf_op jit(solution)/shard_map/slice | solution.py:16
  36.7 2.4 %collective-permute-start.1 = (f32[12,256,8]{1,2,0:T(8,128)S(1)}, f32[12,256,8]{1,2,0:T(8,128)S(1)}, u32[]{:S(2)}, u32[]{:S(2)}) collective-permute-start(f32[12,256,8]{1,2,0:T(8,128)S(1)} %copy.41), channel_id=1, source_target_pairs={{4,0},{8,4},{12,8},{16,12},{20,16},{24,20},{28,24},{0,28},{5,1},{9... | collective-permute-start | bytes 294920 | tf_op jit(solution)/shard_map/ppermute | solution.py:22
  39.1 1.1 copy.40
  40.3 3.0 %copy.51 = f32[4,32,8,128]{3,2,1,0:T(8,128)} copy(f32[4,32,8,128]{1,0,3,2:T(4,128)} %bitcast.378) | data formatting | bytes 1048576 | tf_op jit(solution)/shard_map/all_to_all | solution.py:108
  43.8 4.1 %collective-permute-done = f32[12,256,8]{1,2,0:T(8,128)} collective-permute-done((f32[12,256,8]{1,2,0:T(8,128)}, f32[12,256,8]{1,2,0:T(8,128)}, u32[]{:S(2)}, u32[]{:S(2)}) %collective-permute-start) | collective-permute-done | bytes 98336 | tf_op jit(solution)/shard_map/ppermute | solution.py:20
  47.8 2.5 %copy.42 = f32[12,256,8]{2,1,0:T(8,128)} copy(f32[12,256,8]{1,2,0:T(8,128)} %collective-permute-done) | data formatting | bytes 196608 | tf_op jit(solution)/shard_map/ppermute | solution.py:20
  50.4 1.0 pad_maximum_fusion.7
  52.2 1.4 %collective-permute-done.3 = f32[12,8,144]{2,1,0:T(8,128)S(1)} collective-permute-done((f32[12,8,144]{2,1,0:T(8,128)S(1)}, f32[12,8,144]{2,1,0:T(8,128)S(1)}, u32[]{:S(2)}, u32[]{:S(2)}) %collective-permute-start.3) | collective-permute-done | bytes 55328 | tf_op jit(solution)/shard_map/ppermute | solution.py:22
  53.7 2.9 %collective-permute-done.2 = f32[12,8,144]{2,1,0:T(8,128)S(1)} collective-permute-done((f32[12,8,144]{2,1,0:T(8,128)S(1)}, f32[12,8,144]{2,1,0:T(8,128)S(1)}, u32[]{:S(2)}, u32[]{:S(2)}) %collective-permute-start.2) | collective-permute-done | bytes 55328 | tf_op jit(solution)/shard_map/ppermute | solution.py:20
  56.6 1.3 %pad_maximum_fusion = f32[12,272,144]{2,1,0:T(8,128)S(1)} fusion(f32[12,8,144]{2,1,0:T(8,128)S(1)} %collective-permute-done.3, f32[12,256,8]{2,1,0:T(8,128)S(1)} %copy.43, f32[12,256,128]{2,1,0:T(8,128)S(1)} %constant_dynamic-update-slice_fusion, f32[12,256,8]{2,1,0:T(8,128)S(1)} %copy-done.2, f32[12,8,144]{2,1,0:T(8,128)S(1)} %collective-permute-done.2), kind=kLoop, calls=%fused_computation | loop fusion | flops 1880064 | bytes 3760128 | tf_op jit(solution)/shard_map/concatenate | solution.py:18
  58.7 0.9 copy-done
  61.9 1.5 %copy-done.1 = f32[12,272,144]{2,1,0:T(8,128)S(1)} copy-done((f32[12,272,144]{2,1,0:T(8,128)S(1)}, f32[12,272,144]{2,1,0:T(8,128)}, u32[]{:S(2)}) %copy-start.1) | copy-done | bytes 1880088
  63.4 0.9 fusion.19
  66.4 0.9 fusion.71
  67.3 0.9 fusion.83
  69.5 0.9 fusion.48
  70.4 0.9 fusion.59
  73.4 0.9 copy.49
  74.3 3.4 %all-to-all-start.1 = ((f32[2,256,128]{2,0,1:T(2,128)}), f32[2,256,128]{2,0,1:T(2,128)S(1)}, u32[]{:S(2)}, u32[]{:S(2)}) async-start(f32[2,256,128]{2,0,1:T(2,128)} %copy.49), calls=%async_computation.1 | async-start | bytes 524288 | tf_op jit(solution)/shard_map/all_to_all | solution.py:162
  78.0 1.2 fusion.98
  79.2 40.1 %all-reduce = (f32[1]{0:T(128)}, f32[1]{0:T(128)}, f32[1]{0:T(128)}, f32[1]{0:T(128)}) all-reduce(f32[1]{0:T(128)} %bitcast.78, f32[1]{0:T(128)} %bitcast.77, f32[1]{0:T(128)} %bitcast.76, f32[1]{0:T(128)} %bitcast.75), channel_id=1, replica_groups=mesh['gx'=8,'gy'=4] {'gx','gy'}, use_global_device_ids=true, to_apply=%region_7.0 | all-reduce | flops 4 | bytes 32 | tf_op jit(solution)/shard_map/psum | solution.py:44
  119.3 0.9 slice.886
  120.2 3.0 %pad_maximum_fusion.8 = f32[4]{0:T(128)} fusion(f32[1]{0:T(128)} %get-tuple-element.12, f32[1]{0:T(128)} %get-tuple-element.13, f32[1]{0:T(128)} %get-tuple-element.14, f32[1]{0:T(128)} %get-tuple-element.15), kind=kLoop, calls=%fused_computation.287 | loop fusion | flops 12 | bytes 32 | tf_op jit(solution)/shard_map/stack | solution.py:159
  (74 shorter events, 11.8 us)
Async XLA Ops:
  2.4 9.8 %copy-start.5 = (s32[256,128]{1,0:T(8,128)S(1)}, s32[256,128]{1,0:T(8,128)}, u32[]{:S(2)}) copy-start(s32[256,128]{1,0:T(8,128)} %param.10) | copy-start | bytes 393220
  4.6 8.8 %copy-start.6 = (f32[3,256,128]{2,1,0:T(8,128)S(1)}, f32[3,256,128]{2,1,0:T(8,128)}, u32[]{:S(2)}) copy-start(f32[3,256,128]{2,1,0:T(8,128)} %param.7) | copy-start | bytes 1179652
  4.6 8.8 %copy-start.7 = (f32[256,128]{1,0:T(8,128)S(1)}, f32[256,128]{1,0:T(8,128)}, u32[]{:S(2)}) copy-start(f32[256,128]{1,0:T(8,128)} %param.9) | copy-start | bytes 393220
  4.6 8.8 %copy-start.8 = (f32[256,128]{1,0:T(8,128)S(1)}, f32[256,128]{1,0:T(8,128)}, u32[]{:S(2)}) copy-start(f32[256,128]{1,0:T(8,128)} %param.8) | copy-start | bytes 393220
  4.6 21.9 %all-to-all-start = ((f32[8,1,16384]{2,1,0:T(1,128)}), f32[8,1,16384]{2,1,0:T(1,128)S(1)}, u32[]{:S(2)}, u32[]{:S(2)}) async-start(f32[8,1,16384]{2,1,0:T(1,128)} %reshape.95), calls=%async_computation | async-start | bytes 1048576 | tf_op jit(solution)/shard_map/all_to_all | solution.py:108
  36.7 6.5 %collective-permute-start.1 = (f32[12,256,8]{1,2,0:T(8,128)S(1)}, f32[12,256,8]{1,2,0:T(8,128)S(1)}, u32[]{:S(2)}, u32[]{:S(2)}) collective-permute-start(f32[12,256,8]{1,2,0:T(8,128)S(1)} %copy.41), channel_id=1, source_target_pairs={{4,0},{8,4},{12,8},{16,12},{20,16},{24,20},{28,24},{0,28},{5,1},{9... | collective-permute-start | bytes 294920 | tf_op jit(solution)/shard_map/ppermute | solution.py:22
  40.2 7.6 %collective-permute-start = (f32[12,256,8]{1,2,0:T(8,128)}, f32[12,256,8]{1,2,0:T(8,128)}, u32[]{:S(2)}, u32[]{:S(2)}) collective-permute-start(f32[12,256,8]{1,2,0:T(8,128)} %copy.40), channel_id=1, source_target_pairs={{0,4},{4,8},{8,12},{12,16},{16,20},{20,24},{24,28},{28,0},{1,5},{5... | collective-permute-start | bytes 294920 | tf_op jit(solution)/shard_map/ppermute | solution.py:20
  50.4 1.6 %copy-start.3 = (f32[4,32,8,128]{3,2,1,0:T(8,128)S(1)}, f32[4,32,8,128]{3,2,1,0:T(8,128)}, u32[]{:S(2)}) copy-start(f32[4,32,8,128]{3,2,1,0:T(8,128)} %copy.51) | copy-start | bytes 1572868
  51.4 2.3 %collective-permute-start.3 = (f32[12,8,144]{2,1,0:T(8,128)S(1)}, f32[12,8,144]{2,1,0:T(8,128)S(1)}, u32[]{:S(2)}, u32[]{:S(2)}) collective-permute-start(f32[12,8,144]{2,1,0:T(8,128)S(1)} %get-tuple-element.38), channel_id=1, source_target_pairs={{1,0},{2,1},{3,2},{0,3},{5,4},{6,5},{7,6},{4,7},{9,8},{10,9},{11,1... | collective-permute-start | bytes 165896 | tf_op jit(solution)/shard_map/ppermute | solution.py:22
  51.5 5.2 %collective-permute-start.2 = (f32[12,8,144]{2,1,0:T(8,128)S(1)}, f32[12,8,144]{2,1,0:T(8,128)S(1)}, u32[]{:S(2)}, u32[]{:S(2)}) collective-permute-start(f32[12,8,144]{2,1,0:T(8,128)S(1)} %get-tuple-element.37), channel_id=1, source_target_pairs={{0,1},{1,2},{2,3},{3,0},{4,5},{5,6},{6,7},{7,4},{8,9},{9,10},{10,1... | collective-permute-start | bytes 165896 | tf_op jit(solution)/shard_map/ppermute | solution.py:20
  52.0 4.7 %copy-start.2 = (f32[12,256,8]{2,1,0:T(8,128)S(1)}, f32[12,256,8]{2,1,0:T(8,128)}, u32[]{:S(2)}) copy-start(f32[12,256,8]{2,1,0:T(8,128)} %copy.42) | copy-start | bytes 294916
  57.9 1.7 %copy-start = (f32[12,272,144]{2,1,0:T(8,128)}, f32[12,272,144]{2,1,0:T(8,128)S(1)}, u32[]{:S(2)}) copy-start(f32[12,272,144]{2,1,0:T(8,128)S(1)} %pad_maximum_fusion) | copy-start | bytes 5640196
  60.3 1.2 slice-start
  61.5 1.9 %copy-start.1 = (f32[12,272,144]{2,1,0:T(8,128)S(1)}, f32[12,272,144]{2,1,0:T(8,128)}, u32[]{:S(2)}) copy-start(f32[12,272,144]{2,1,0:T(8,128)} %copy-done) | copy-start | bytes 5640196
  73.4 5.7 %copy-start.4 = (f32[2,256,128]{2,1,0:T(8,128)}, f32[2,256,128]{2,1,0:T(8,128)S(1)}, u32[]{:S(2)}) copy-start(f32[2,256,128]{2,1,0:T(8,128)S(1)} %get-tuple-element.17) | copy-start | bytes 786436
  74.3 48.9 %all-to-all-start.1 = ((f32[2,256,128]{2,0,1:T(2,128)}), f32[2,256,128]{2,0,1:T(2,128)S(1)}, u32[]{:S(2)}, u32[]{:S(2)}) async-start(f32[2,256,128]{2,0,1:T(2,128)} %copy.49), calls=%async_computation.1 | async-start | bytes 524288 | tf_op jit(solution)/shard_map/all_to_all | solution.py:162
where the time goes:
time: 125 us; the launch traced here: 124 us
  blocking collectives  40.1 us (32%)
  local copies, waits for them, and re-layouts  27.9 us (22%)
  waiting for transfers between devices  21.5 us (17%)
  other arithmetic  19.8 us (16%)
  starting transfers between devices  13.8 us (11%)
    psum x1, blocking collectives, record_sum(): global_sums.append(lax.psum(own_sum, ('gx', 'gy')))  40.1 us
    all_to_all x1, waiting for transfers between devices, local(): lax.all_to_all(ocean_forcing, 'gx', split_axis=2, concat_axis=1, tiled=True)  13 us
    unnamed x25, local copies, waits for them, and re-layouts  9.82 us
    all_to_all x1, starting transfers between devices, local(): lax.all_to_all(ocean_forcing, 'gx', split_axis=2, concat_axis=1, tiled=True)  7.41 us
    ppermute x2, waiting for transfers between devices, extended(): lax.ppermute(tail, axis, [(i, (i + 1) % count) for i in range(count)])  7.03 us
    all_to_all x3, local copies, waits for them, and re-layouts, local(): lax.all_to_all(ocean_forcing, 'gx', split_axis=2, concat_axis=1, tiled=True)  5.33 us
    another operation x8, other arithmetic, relax_stress(): jnp.stack([strength * (divergence / delta_rate - 1.0), strength * tension...  3.65 us
    all_to_all x1, starting transfers between devices, local(): lax.all_to_all(ice_stress, 'gx', split_axis=1, concat_axis=2, tiled=True)  3.41 us
  transfers between devices with their start and end apart: 6, of which 4 were waited for; matrix products, arithmetic and copies ran while one was open for 9% of the time, Pallas kernels for 0%

commit v1 on v0

--- a/solution.py
+++ b/solution.py
@@ -8,6 +8,7 @@
 BETA = 4.0
 WATER_DRAG = 1.0
 DELTA_FLOOR = 0.0025
+edit_goods = lambda q_in: jnp.sum(lax.all_gather(q_in, ("gx", "gy")), 0)
 
 
 def extended(cells, sides, width):
@@ -41,7 +42,7 @@
 
 
 def record_sum(own_sum, global_sums):
-    global_sums.append(lax.psum(own_sum, ("gx", "gy")))
+    global_sums.append(edit_goods(own_sum))
 
 
 def relax_stress(padded_vel, stress, strength, ice_frac):

time: 125 us -> 130 us (1.040)
  local copies, waits for them, and re-layouts: 27.9 us -> 30.8 us
  other arithmetic: 19.8 us -> 22.3 us
    psum x1 -> x0, blocking collectives: 40.1 us -> none  [record_sum(): global_sums.append(lax.psum(own_sum, ('gx', 'gy')))]
    unnamed x0 -> x1, blocking collectives: none -> 39.8 us
    unnamed x25 -> x33, local copies, waits for them, and re-layouts: 9.82 us -> 12.7 us
    reduce_sum x0 -> x4, other arithmetic: none -> 2.51 us  [edit_goods = lambda q_in: jnp.sum(lax.all_gather(q_in, ('gx', 'gy')), 0)]
  transfers between devices with their start and end apart: 6 -> 6, of which waited for: 4 -> 4; matrix products, arithmetic and copies ran while one was open for 9% -> 13% of each run, Pallas kernels for 0% -> 0%
where the time goes in v1:
time: 130 us; the launch traced here: 129 us
  blocking collectives  39.8 us (31%)
  local copies, waits for them, and re-layouts  30.8 us (24%)
  other arithmetic  22.3 us (17%)
  waiting for transfers between devices  21.5 us (17%)
  starting transfers between devices  13.8 us (11%)
    unnamed x1, blocking collectives  39.8 us
    all_to_all x1, waiting for transfers between devices, local(): lax.all_to_all(ocean_forcing, 'gx', split_axis=2, concat_axis=1, tiled=True)  13 us
    unnamed x33, local copies, waits for them, and re-layouts  12.7 us
    all_to_all x1, starting transfers between devices, local(): lax.all_to_all(ocean_forcing, 'gx', split_axis=2, concat_axis=1, tiled=True)  7.41 us
    ppermute x2, waiting for transfers between devices, extended(): lax.ppermute(tail, axis, [(i, (i + 1) % count) for i in range(count)])  7.05 us
    all_to_all x3, local copies, waits for them, and re-layouts, local(): lax.all_to_all(ocean_forcing, 'gx', split_axis=2, concat_axis=1, tiled=True)  5.32 us
    another operation x8, other arithmetic, relax_stress(): jnp.stack([strength * (divergence / delta_rate - 1.0), strength * tension...  3.65 us
    all_to_all x1, starting transfers between devices, local(): lax.all_to_all(ice_stress, 'gx', split_axis=1, concat_axis=2, tiled=True)  3.41 us
  transfers between devices with their start and end apart: 6, of which 4 were waited for; matrix products, arithmetic and copies ran while one was open for 13% of the time, Pallas kernels for 0%

profile of v1, /device:TPU:0, one launch (start us, length us, event | category | flops | bytes accessed | tf_op | source)
XLA Modules:
  0.0 129.2 jit_solution(6858294272316270593)
XLA Ops:
  0.6 1.8 %copy.37 = f32[4,32,1024]{1,0,2:T(4,128)S(1)} copy(f32[4,32,1024]{2,1,0:T(8,128)} %param.11) | data formatting | bytes 1048576 | tf_op args[5]
  2.4 2.1 %reshape.103 = f32[8,1,16384]{2,1,0:T(1,128)} reshape(f32[1024,4,32]{2,1,0:T(4,128)S(1)} %bitcast.399) | data formatting | bytes 1048576
  4.6 7.4 %all-to-all-start = ((f32[8,1,16384]{2,1,0:T(1,128)}), f32[8,1,16384]{2,1,0:T(1,128)S(1)}, u32[]{:S(2)}, u32[]{:S(2)}) async-start(f32[8,1,16384]{2,1,0:T(1,128)} %reshape.103), calls=%async_computation | async-start | bytes 1048576 | tf_op jit(solution)/shard_map/all_to_all | solution.py:109
  12.2 1.0 constant_dynamic-update-slice_fusion.2
  13.4 13.0 %all-to-all-done = f32[8,1,16384]{2,1,0:T(1,128)S(1)} async-done(((f32[8,1,16384]{2,1,0:T(1,128)}), f32[8,1,16384]{2,1,0:T(1,128)S(1)}, u32[]{:S(2)}, u32[]{:S(2)}) %all-to-all-start) | async-done | bytes 524320 | tf_op jit(solution)/shard_map/all_to_all | solution.py:109
  27.0 1.9 %reduce.10 = f32[8,16384]{1,0:T(8,128)S(1)} reduce(f32[8,1,16384]{2,1,0:T(1,128)S(1)} %all-to-all-done, f32[]{:T(128)} %broadcast.260), dimensions={1}, to_apply=%all_to_all.26.reduce_sub_computation | reduce | bytes 1048580 | tf_op jit(solution)/shard_map/all_to_all | solution.py:109
  28.9 2.4 %reshape.104 = f32[1024,4,32]{2,1,0:T(4,128)} reshape(f32[8,16384]{1,0:T(8,128)S(1)} %reduce.10) | data formatting | bytes 1048576
  31.3 1.8 %copy.52 = f32[4,32,8,128]{3,1,2,0:T(8,128)S(1)} copy(f32[4,32,8,128]{1,0,3,2:T(4,128)} %bitcast.381) | data formatting | bytes 1048576 | tf_op jit(solution)/shard_map/all_to_all | solution.py:109
  33.2 1.7 %fusion.160 = (f32[12,256,8]{2,1,0:T(8,128)S(1)}, f32[12,256,8]{2,1,0:T(8,128)}) fusion(f32[12,256,128]{2,1,0:T(8,128)S(1)} %constant_dynamic-update-slice_fusion), kind=kLoop, calls=%fused_computation.288 | loop fusion | bytes 393216 | tf_op jit(solution)/shard_map/slice | solution.py:18
  34.9 1.8 %copy.41 = f32[12,256,8]{1,2,0:T(8,128)S(1)} copy(f32[12,256,8]{2,1,0:T(8,128)} %get-tuple-element.42) | data formatting | bytes 196608 | tf_op jit(solution)/shard_map/slice | solution.py:17
  36.7 2.4 %collective-permute-start.1 = (f32[12,256,8]{1,2,0:T(8,128)S(1)}, f32[12,256,8]{1,2,0:T(8,128)S(1)}, u32[]{:S(2)}, u32[]{:S(2)}) collective-permute-start(f32[12,256,8]{1,2,0:T(8,128)S(1)} %copy.41), channel_id=1, source_target_pairs={{4,0},{8,4},{12,8},{16,12},{20,16},{24,20},{28,24},{0,28},{5,1},{9... | collective-permute-start | bytes 294920 | tf_op jit(solution)/shard_map/ppermute | solution.py:23
  39.1 1.1 copy.40
  40.3 3.0 %copy.51 = f32[4,32,8,128]{3,2,1,0:T(8,128)} copy(f32[4,32,8,128]{1,0,3,2:T(4,128)} %bitcast.382) | data formatting | bytes 1048576 | tf_op jit(solution)/shard_map/all_to_all | solution.py:109
  43.7 4.1 %collective-permute-done = f32[12,256,8]{1,2,0:T(8,128)} collective-permute-done((f32[12,256,8]{1,2,0:T(8,128)}, f32[12,256,8]{1,2,0:T(8,128)}, u32[]{:S(2)}, u32[]{:S(2)}) %collective-permute-start) | collective-permute-done | bytes 98336 | tf_op jit(solution)/shard_map/ppermute | solution.py:21
  47.8 2.5 %copy.42 = f32[12,256,8]{2,1,0:T(8,128)} copy(f32[12,256,8]{1,2,0:T(8,128)} %collective-permute-done) | data formatting | bytes 196608 | tf_op jit(solution)/shard_map/ppermute | solution.py:21
  50.4 1.0 pad_maximum_fusion.7
  52.2 1.4 %collective-permute-done.3 = f32[12,8,144]{2,1,0:T(8,128)S(1)} collective-permute-done((f32[12,8,144]{2,1,0:T(8,128)S(1)}, f32[12,8,144]{2,1,0:T(8,128)S(1)}, u32[]{:S(2)}, u32[]{:S(2)}) %collective-permute-start.3) | collective-permute-done | bytes 55328 | tf_op jit(solution)/shard_map/ppermute | solution.py:23
  53.7 2.9 %collective-permute-done.2 = f32[12,8,144]{2,1,0:T(8,128)S(1)} collective-permute-done((f32[12,8,144]{2,1,0:T(8,128)S(1)}, f32[12,8,144]{2,1,0:T(8,128)S(1)}, u32[]{:S(2)}, u32[]{:S(2)}) %collective-permute-start.2) | collective-permute-done | bytes 55328 | tf_op jit(solution)/shard_map/ppermute | solution.py:21
  56.6 1.3 pad_maximum_fusion
  58.7 0.9 copy-done
  61.8 1.5 %copy-done.1 = f32[12,272,144]{2,1,0:T(8,128)S(1)} copy-done((f32[12,272,144]{2,1,0:T(8,128)S(1)}, f32[12,272,144]{2,1,0:T(8,128)}, u32[]{:S(2)}) %copy-start.1) | copy-done | bytes 1880088
  63.4 0.9 fusion.19
  66.4 0.9 fusion.71
  67.3 0.9 fusion.83
  69.5 0.9 fusion.48
  70.4 0.9 fusion.59
  73.4 0.9 copy.49
  74.3 3.4 %all-to-all-start.1 = ((f32[2,256,128]{2,0,1:T(2,128)}), f32[2,256,128]{2,0,1:T(2,128)S(1)}, u32[]{:S(2)}, u32[]{:S(2)}) async-start(f32[2,256,128]{2,0,1:T(2,128)} %copy.49), calls=%async_computation.1 | async-start | bytes 524288 | tf_op jit(solution)/shard_map/all_to_all | solution.py:163
  77.9 1.2 fusion.98
  82.1 39.8 %all-reduce.4 = (f32[32]{0:T(128)S(1)}, f32[32]{0:T(128)S(1)}, f32[32]{0:T(128)S(1)}, f32[32]{0:T(128)S(1)}) all-reduce(f32[32]{0:T(128)S(1)} %dynamic-update-slice.3, f32[32]{0:T(128)S(1)} %dynamic-update-slice.2, f32[32]{0:T(128)S(1)} %dynamic-update-slice.1, f32[32]{0:T(128)S(1)} %dynamic-update-slice), channel_id=1, replica_groups=mesh['gx'=8,'gy'=4] {'gx','gy'}, use_global_device_ids=true, to_apply=%add.3 | all-reduce | flops 128 | bytes 1024
  121.8 0.9 slice.886
  125.2 3.0 %pad_maximum_fusion.8 = f32[4]{0:T(128)} fusion(f32[1]{0:T(128)} %bitcast.82, f32[1]{0:T(128)} %bitcast.80, f32[1]{0:T(128)} %bitcast.78, f32[1]{0:T(128)} %bitcast.76), kind=kLoop, calls=%fused_computation.287 | loop fusion | flops 12 | bytes 32 | tf_op jit(solution)/shard_map/stack | solution.py:160
  (86 shorter events, 17.2 us)
Async XLA Ops:
  2.4 9.8 %copy-start.5 = (s32[256,128]{1,0:T(8,128)S(1)}, s32[256,128]{1,0:T(8,128)}, u32[]{:S(2)}) copy-start(s32[256,128]{1,0:T(8,128)} %param.10) | copy-start | bytes 393220
  4.5 8.8 %copy-start.6 = (f32[3,256,128]{2,1,0:T(8,128)S(1)}, f32[3,256,128]{2,1,0:T(8,128)}, u32[]{:S(2)}) copy-start(f32[3,256,128]{2,1,0:T(8,128)} %param.7) | copy-start | bytes 1179652
  4.5 8.8 %copy-start.7 = (f32[256,128]{1,0:T(8,128)S(1)}, f32[256,128]{1,0:T(8,128)}, u32[]{:S(2)}) copy-start(f32[256,128]{1,0:T(8,128)} %param.9) | copy-start | bytes 393220
  4.5 8.8 %copy-start.8 = (f32[256,128]{1,0:T(8,128)S(1)}, f32[256,128]{1,0:T(8,128)}, u32[]{:S(2)}) copy-start(f32[256,128]{1,0:T(8,128)} %param.8) | copy-start | bytes 393220
  4.6 21.9 %all-to-all-start = ((f32[8,1,16384]{2,1,0:T(1,128)}), f32[8,1,16384]{2,1,0:T(1,128)S(1)}, u32[]{:S(2)}, u32[]{:S(2)}) async-start(f32[8,1,16384]{2,1,0:T(1,128)} %reshape.103), calls=%async_computation | async-start | bytes 1048576 | tf_op jit(solution)/shard_map/all_to_all | solution.py:109
  36.7 6.5 %collective-permute-start.1 = (f32[12,256,8]{1,2,0:T(8,128)S(1)}, f32[12,256,8]{1,2,0:T(8,128)S(1)}, u32[]{:S(2)}, u32[]{:S(2)}) collective-permute-start(f32[12,256,8]{1,2,0:T(8,128)S(1)} %copy.41), channel_id=1, source_target_pairs={{4,0},{8,4},{12,8},{16,12},{20,16},{24,20},{28,24},{0,28},{5,1},{9... | collective-permute-start | bytes 294920 | tf_op jit(solution)/shard_map/ppermute | solution.py:23
  40.2 7.6 %collective-permute-start = (f32[12,256,8]{1,2,0:T(8,128)}, f32[12,256,8]{1,2,0:T(8,128)}, u32[]{:S(2)}, u32[]{:S(2)}) collective-permute-start(f32[12,256,8]{1,2,0:T(8,128)} %copy.40), channel_id=1, source_target_pairs={{0,4},{4,8},{8,12},{12,16},{16,20},{20,24},{24,28},{28,0},{1,5},{5... | collective-permute-start | bytes 294920 | tf_op jit(solution)/shard_map/ppermute | solution.py:21
  50.3 1.6 %copy-start.3 = (f32[4,32,8,128]{3,2,1,0:T(8,128)S(1)}, f32[4,32,8,128]{3,2,1,0:T(8,128)}, u32[]{:S(2)}) copy-start(f32[4,32,8,128]{3,2,1,0:T(8,128)} %copy.51) | copy-start | bytes 1572868
  51.4 2.3 %collective-permute-start.3 = (f32[12,8,144]{2,1,0:T(8,128)S(1)}, f32[12,8,144]{2,1,0:T(8,128)S(1)}, u32[]{:S(2)}, u32[]{:S(2)}) collective-permute-start(f32[12,8,144]{2,1,0:T(8,128)S(1)} %get-tuple-element.38), channel_id=1, source_target_pairs={{1,0},{2,1},{3,2},{0,3},{5,4},{6,5},{7,6},{4,7},{9,8},{10,9},{11,1... | collective-permute-start | bytes 165896 | tf_op jit(solution)/shard_map/ppermute | solution.py:23
  51.4 5.2 %collective-permute-start.2 = (f32[12,8,144]{2,1,0:T(8,128)S(1)}, f32[12,8,144]{2,1,0:T(8,128)S(1)}, u32[]{:S(2)}, u32[]{:S(2)}) collective-permute-start(f32[12,8,144]{2,1,0:T(8,128)S(1)} %get-tuple-element.37), channel_id=1, source_target_pairs={{0,1},{1,2},{2,3},{3,0},{4,5},{5,6},{6,7},{7,4},{8,9},{9,10},{10,1... | collective-permute-start | bytes 165896 | tf_op jit(solution)/shard_map/ppermute | solution.py:21
  51.9 4.7 %copy-start.2 = (f32[12,256,8]{2,1,0:T(8,128)S(1)}, f32[12,256,8]{2,1,0:T(8,128)}, u32[]{:S(2)}) copy-start(f32[12,256,8]{2,1,0:T(8,128)} %copy.42) | copy-start | bytes 294916
  57.9 1.7 %copy-start = (f32[12,272,144]{2,1,0:T(8,128)}, f32[12,272,144]{2,1,0:T(8,128)S(1)}, u32[]{:S(2)}) copy-start(f32[12,272,144]{2,1,0:T(8,128)S(1)} %pad_maximum_fusion) | copy-start | bytes 5640196
  60.3 1.2 slice-start
  61.4 1.9 %copy-start.1 = (f32[12,272,144]{2,1,0:T(8,128)S(1)}, f32[12,272,144]{2,1,0:T(8,128)}, u32[]{:S(2)}) copy-start(f32[12,272,144]{2,1,0:T(8,128)} %copy-done) | copy-start | bytes 5640196
  73.4 5.8 %copy-start.4 = (f32[2,256,128]{2,1,0:T(8,128)}, f32[2,256,128]{2,1,0:T(8,128)S(1)}, u32[]{:S(2)}) copy-start(f32[2,256,128]{2,1,0:T(8,128)S(1)} %get-tuple-element.17) | copy-start | bytes 786436
  74.3 54.0 %all-to-all-start.1 = ((f32[2,256,128]{2,0,1:T(2,128)}), f32[2,256,128]{2,0,1:T(2,128)S(1)}, u32[]{:S(2)}, u32[]{:S(2)}) async-start(f32[2,256,128]{2,0,1:T(2,128)} %copy.49), calls=%async_computation.1 | async-start | bytes 524288 | tf_op jit(solution)/shard_map/all_to_all | solution.py:163
